TPU v7x, 32 devices: a whole 2x2x4 slice. The times are simulated.
32 devices in a mesh: dp: 4 (over x, core), half: 2 (over y), own: 4 (over z).
Axes of the slice: x: 2, y: 2, z: 4, core: 2. Of those that a mesh axis runs over, the one named last changes fastest.
Arguments:
- grad_parts: bfloat16 [4, 6, 1024, 1024], P('dp', None, ('half', 'own')), may hold values from -6 to 6
- owner_table: int32 [6, 1], replicated, may hold values from 0 to 3; in each aligned block of 6 rows (0 to 5, 6 to 11, ...) at most 2 rows name the same one
- left_basis: bfloat16 [8, 1024, 1024], P(('half', 'own')), may hold values from -0.1875 to 0.1875
- right_basis: bfloat16 [8, 1024, 1024], P(('half', 'own')), may hold values from -0.1875 to 0.1875
- first_moment: bfloat16 [8, 1024, 1024], P(('half', 'own'), 'dp'), may hold values from -6 to 6
- second_moment: bfloat16 [8, 1024, 1024], P(('half', 'own'), 'dp'), may hold values from 0.5 to 8
Outputs:
- update: bfloat16 [6, 1024, 1024], P(None, ('half', 'own'), 'dp')
Inputs may be any that keep to these rules, and one draw needn't show every extreme that they name: `owner_table`: every owner index is named by at least one block and by at most 2 blocks; some owner is named by exactly 2 blocks.
All inputs are finite; a program needn't handle non-finite values.
Results may differ from a plain program's by a relative error of at most 0.013.
Values may be sent and summed in bfloat16 or wider, within the bound.
A program may use at most 128 MiB of HBM per device.

v0:
```python
import jax
import jax.numpy as jnp
from jax import lax
from jax.sharding import PartitionSpec as P

beta_first = 0.9
beta_second = 0.95
bias_first = 1.0 - 0.9**10
bias_second = 1.0 - 0.95**10
epsilon = 1e-08


def slot_select(owner_table, owner_count, slot_count):
    owner_ids = owner_table[:, 0]
    positions = jnp.arange(owner_ids.shape[0], dtype=jnp.int32)
    shared = (owner_ids[:, None] == owner_ids[None, :]) & (positions[None, :] < positions[:, None])
    ranking = jnp.sum(shared.astype(jnp.int32), axis=1)
    slot_ids = ranking * owner_count + owner_ids
    slot_range = jnp.arange(slot_count, dtype=jnp.int32)
    return (slot_range[:, None] == slot_ids[None, :]).astype(jnp.bfloat16)


def local(grad_parts, owner_table, left_basis, right_basis, first_moment, second_moment):
    halves = lax.axis_size("half")
    owners = lax.axis_size("own")
    replicas = lax.axis_size("dp")
    block_count = grad_parts.shape[1]
    piece_rows = grad_parts.shape[2]
    block_width = grad_parts.shape[3]
    quarter = block_width // replicas
    offset = lax.axis_index("dp") * quarter
    summed = lax.psum_scatter(
        grad_parts[0].astype(jnp.float32).astype(jnp.bfloat16),
        "dp",
        scatter_dimension=2,
        tiled=True,
    )
    selector = slot_select(owner_table, owners, halves * owners)
    flat_grad = summed.reshape(block_count, piece_rows * quarter)
    packed = jnp.dot(selector, flat_grad, preferred_element_type=jnp.float32).astype(jnp.bfloat16)
    packed = packed.reshape(halves, owners, piece_rows, quarter)
    arrived = lax.all_to_all(
        lax.all_to_all(packed, "half", split_axis=0, concat_axis=0, tiled=True),
        "own",
        split_axis=1,
        concat_axis=1,
        tiled=True,
    )
    grad_block = arrived.reshape(block_width, quarter)
    left_matrix = left_basis[0]
    right_matrix = right_basis[0]
    right_rows = lax.dynamic_slice_in_dim(right_matrix, offset, quarter, 0)
    left_slice = lax.dynamic_slice_in_dim(left_matrix, offset, quarter, 1)
    projected = lax.dot_general(
        left_slice,
        lax.all_gather(grad_block, "dp", axis=1, tiled=True),
        (((0,), (0,)), ((), ())),
        preferred_element_type=jnp.float32,
    )
    rotated = jnp.dot(
        projected.astype(jnp.bfloat16), right_matrix, preferred_element_type=jnp.float32
    )
    first_new = beta_first * first_moment[0].astype(jnp.float32) + (1.0 - beta_first) * rotated
    second_new = (
        beta_second * second_moment[0].astype(jnp.float32) + (1.0 - beta_second) * rotated * rotated
    )
    direction = (first_new / bias_first / (jnp.sqrt(second_new / bias_second) + epsilon)).astype(
        jnp.bfloat16
    )
    partial_cols = lax.dot_general(
        lax.all_gather(direction, "dp", axis=0, tiled=True),
        right_rows,
        (((1,), (1,)), ((), ())),
        preferred_element_type=jnp.float32,
    )
    update_block = jnp.dot(
        left_matrix, partial_cols.astype(jnp.bfloat16), preferred_element_type=jnp.float32
    )
    outgoing = update_block.astype(jnp.bfloat16).reshape(halves, owners, piece_rows, quarter)
    returned = lax.all_to_all(
        lax.all_to_all(outgoing, "half", split_axis=0, concat_axis=0, tiled=True),
        "own",
        split_axis=1,
        concat_axis=1,
        tiled=True,
    )
    flat_back = returned.reshape(halves * owners, piece_rows * quarter)
    placed = lax.dot_general(
        selector, flat_back, (((0,), (0,)), ((), ())), preferred_element_type=jnp.float32
    )
    return placed.astype(jnp.bfloat16).reshape(block_count, piece_rows, quarter)


def solution(mesh):
    return jax.shard_map(
        local,
        mesh=mesh,
        in_specs=(
            P("dp", None, ("half", "own"), None),
            P(),
            P(("half", "own"), None, None),
            P(("half", "own"), None, None),
            P(("half", "own"), "dp", None),
            P(("half", "own"), "dp", None),
        ),
        out_specs=P(None, ("half", "own"), "dp"),
        check_vma=False,
    )
```

profile of v0, /device:TPU:0, one launch (start us, length us, event | category | flops | bytes accessed | tf_op | source)
XLA Modules:
  0.0 161.1 jit_solution(16821739264425904918)
XLA Ops:
  6.5 0.0 copy-start
  6.5 0.0 reduce-scatter.2.cloned.1.call-start
  6.5 0.7 reduce-scatter.2.cloned.1.call-update
  7.3 0.0 all-gather.3.cloned.1.call-start
  7.3 0.9 convert_reduce_fusion
  8.2 0.7 multiply_add_fusion
  8.9 31.8 %reduce-scatter.2.cloned.1.call-done = bf16[6,128,256]{2,1,0:T(8,128)(2,1)} async-done(((bf16[6,128,1024]{2,1,0:T(8,128)(2,1)}), bf16[6,128,256]{2,1,0:T(8,128)(2,1)}) %reduce-scatter.2.cloned.1.call-update) | async-done | bytes 393232 | tf_op jit(solution)/shard_map/reduce_scatter | solution.py:32
  40.7 1.2 copy.26
  41.9 0.3 convolution_convert_fusion.1
  42.2 0.1 copy.27
  42.3 10.5 %all_to_all.20 = bf16[2,4,128,256]{3,2,1,0:T(8,128)(2,1)S(1)} all-to-all(bf16[2,4,128,256]{3,2,1,0:T(8,128)(2,1)S(1)} %bitcast.60), channel_id=1, replica_groups=mesh['dp'=4,'half'=2,'own'=4] {'half'}, dimensions={0} | all-to-all | bytes 1048576 | tf_op jit(solution)/shard_map/all_to_all | solution.py:43
  52.8 0.0 copy-start.1
  52.8 0.0 copy-start.2
  52.8 17.9 %all_to_all.21 = bf16[2,4,128,256]{3,2,0,1:T(8,128)(2,1)S(1)} all-to-all(bf16[2,4,128,256]{3,2,0,1:T(8,128)(2,1)S(1)} %copy.20), channel_id=1, replica_groups=mesh['dp'=4,'half'=2,'own'=4] {'own'}, dimensions={1} | all-to-all | bytes 1048576 | tf_op jit(solution)/shard_map/all_to_all | solution.py:42
  70.7 0.8 copy.21
  71.6 0.0 all-gather.3.cloned.1.call-update
  71.6 0.0 all-gather.5.cloned.1.call-start
  71.6 20.2 %all-gather.3.cloned.1.call-done = bf16[1024,1024]{1,0:T(8,128)(2,1)} async-done(((bf16[1024,256]{1,0:T(8,128)(2,1)}), bf16[1024,1024]{1,0:T(8,128)(2,1)}) %all-gather.3.cloned.1.call-update) | async-done | bytes 2097168 | tf_op jit(solution)/shard_map/all_gather | solution.py:56
  91.8 0.0 copy-done
  91.8 0.0 copy-done.1
  91.8 0.0 copy-done.2
  91.8 5.0 %fusion.16 = bf16[256,1024]{1,0:T(8,128)(2,1)} fusion(bf16[1,256,1024]{2,1,0:T(8,128)(2,1)S(1)} %copy-done.1, bf16[1,256,1024]{2,1,0:T(8,128)(2,1)S(1)} %copy-done.2, bf16[1,1024,1024]{2,1,0:T(8,128)(2,1)} %param.9, bf16[1024,1024]{1,0:T(8,128)(2,1)} %all-gather.3.cloned.1.call-done, bf16[1,1024,1024]{2,1,0:T(8,128)(2,1)S(1)} %copy-done, s32[]{:T(128)S(6)} %select_n.4), kind=kOutput, calls=%fused_computation.18 | convolution fusion | flops 1077673984 | bytes 6291460 | tf_op jit(solution)/shard_map/dot_general | solution.py:60
  96.8 0.0 all-gather.5.cloned.1.call-update
  96.8 22.7 %all-gather.5.cloned.1.call-done = bf16[1024,1024]{1,0:T(8,128)(2,1)} async-done(((bf16[256,1024]{1,0:T(8,128)(2,1)}), bf16[1024,1024]{1,0:T(8,128)(2,1)}) %all-gather.5.cloned.1.call-update) | async-done | bytes 2097168 | tf_op jit(solution)/shard_map/all_gather | solution.py:71
  119.5 4.0 %fusion.7 = bf16[1024,256]{0,1:T(8,128)(2,1)S(1)} fusion(bf16[1,1024,1024]{2,1,0:T(8,128)(2,1)S(1)} %copy-done, bf16[1024,1024]{1,0:T(8,128)(2,1)} %all-gather.5.cloned.1.call-done, bf16[1,1024,1024]{2,1,0:T(8,128)(2,1)} %param.9, s32[]{:T(128)S(6)} %select_n.4), kind=kOutput, calls=%fused_computation.10 | convolution fusion | flops 1074266112 | bytes 5242884 | tf_op jit(solution)/shard_map/dot_general | solution.py:76
  123.5 0.2 copy.25
  123.7 11.1 %all_to_all.22 = bf16[2,4,128,256]{3,2,1,0:T(8,128)(2,1)S(1)} all-to-all(bf16[2,4,128,256]{3,2,1,0:T(8,128)(2,1)S(1)} %bitcast.61), channel_id=1, replica_groups=mesh['dp'=4,'half'=2,'own'=4] {'half'}, dimensions={0} | all-to-all | bytes 1048576 | tf_op jit(solution)/shard_map/all_to_all | solution.py:81
  134.8 18.3 %all_to_all.23 = bf16[2,4,128,256]{3,2,0,1:T(8,128)(2,1)S(1)} all-to-all(bf16[2,4,128,256]{3,2,0,1:T(8,128)(2,1)S(1)} %copy.23), channel_id=1, replica_groups=mesh['dp'=4,'half'=2,'own'=4] {'own'}, dimensions={1} | all-to-all | bytes 1048576 | tf_op jit(solution)/shard_map/all_to_all | solution.py:80
  153.1 0.3 copy.28
  153.4 0.4 convolution_convert_fusion
  153.8 0.8 copy.31
  (3 shorter events, 0.1 us)
Async XLA Ops:
  6.5 85.3 %copy-start = (bf16[1,1024,1024]{2,1,0:T(8,128)(2,1)S(1)}, bf16[1,1024,1024]{2,1,0:T(8,128)(2,1)}, u32[]{:S(2)}) copy-start(bf16[1,1024,1024]{2,1,0:T(8,128)(2,1)} %param.8) | copy-start | bytes 6291460
  6.5 34.1 %reduce-scatter.2.cloned.1.call-start = ((), (), s32[]{:S(2)}) async-start(), calls=%async_computation.5 | async-start | bytes 1966080 | tf_op jit(solution)/shard_map/reduce_scatter | solution.py:32
  7.3 84.6 %all-gather.3.cloned.1.call-start = ((), (), s32[]{:S(2)}) async-start(), calls=%async_computation.6 | async-start | bytes 2621440 | tf_op jit(solution)/shard_map/all_gather | solution.py:56
  52.8 39.0 %copy-start.1 = (bf16[1,256,1024]{2,1,0:T(8,128)(2,1)S(1)}, bf16[1,256,1024]{2,1,0:T(8,128)(2,1)}, u32[]{:S(2)}) copy-start(bf16[1,256,1024]{2,1,0:T(8,128)(2,1)} %param.11) | copy-start | bytes 1572868
  52.8 39.0 %copy-start.2 = (bf16[1,256,1024]{2,1,0:T(8,128)(2,1)S(1)}, bf16[1,256,1024]{2,1,0:T(8,128)(2,1)}, u32[]{:S(2)}) copy-start(bf16[1,256,1024]{2,1,0:T(8,128)(2,1)} %param.10) | copy-start | bytes 1572868
  71.6 47.9 %all-gather.5.cloned.1.call-start = ((), (), s32[]{:S(2)}) async-start(), calls=%async_computation.7 | async-start | bytes 2621440 | tf_op jit(solution)/shard_map/all_gather | solution.py:71
Sparse Core Ops, SparseCore 0:
  9.9 30.7 reduce-scatter.1
  71.7 20.0 all-gather.2
  96.9 22.5 all-gather.4
where the time goes:
time: 162 us; the launch traced here: 161 us
  waiting for transfers between devices  75.4 us (47%)
  blocking collectives  57.7 us (36%)
  between operations  13.2 us (8%)
  matrix products  9.55 us (6%)
  local copies, waits for them, and re-layouts  3.59 us (2%)
    reduce_scatter x1, waiting for transfers between devices, local(): lax.psum_scatter(grad_parts[0].astype(jnp.float32).astype(jnp.bfloat16),...  31.8 us
    all_gather x1, waiting for transfers between devices, local(): lax.all_gather(direction, 'dp', axis=0, tiled=True)  22.7 us
    all_gather x1, waiting for transfers between devices, local(): lax.all_gather(grad_block, 'dp', axis=1, tiled=True)  20.2 us
    all_to_all x1, blocking collectives, local(): lax.all_to_all(lax.all_to_all(outgoing, 'half', split_axis=0, concat_axis...  18.3 us
    all_to_all x1, blocking collectives, local(): lax.all_to_all(lax.all_to_all(packed, 'half', split_axis=0, concat_axis=0...  17.9 us
    all_to_all x1, blocking collectives, local(): lax.all_to_all(outgoing, 'half', split_axis=0, concat_axis=0, tiled=True)  11.1 us
    all_to_all x1, blocking collectives, local(): lax.all_to_all(packed, 'half', split_axis=0, concat_axis=0, tiled=True)  10.5 us
    dot_general x1, matrix products, local(): jnp.dot(projected.astype(jnp.bfloat16), right_matrix, preferred_element_t...  4.95 us
  transfers between devices with their start and end apart: 3, of which 3 were waited for; matrix products, arithmetic and copies ran while one was open for 1% of the time, Pallas kernels for 0%

commit v1 on v0

--- a/solution.py
+++ b/solution.py
@@ -1,6 +1,10 @@
+import functools
+
 import jax
 import jax.numpy as jnp
 from jax import lax
+from jax.experimental import pallas as pl
+from jax.experimental.pallas import tpu as pltpu
 from jax.sharding import PartitionSpec as P
 
 beta_first = 0.9
@@ -91,9 +95,427 @@
     return placed.astype(jnp.bfloat16).reshape(block_count, piece_rows, quarter)
 
 
+MESH = pl.DeviceIdType.MESH
+LANES = 128
+TILE_ROWS = 16
+
+
+def pick(index, values):
+    chosen = values[0]
+    for i in range(1, len(values)):
+        chosen = lax.select_n(index == i, chosen, values[i])
+    return chosen
+
+
+def step_kernel(
+    sizes,
+    table,
+    grad,
+    left_in,
+    right_in,
+    first_in,
+    second_in,
+    out,
+    left,
+    right,
+    first,
+    second,
+    own,
+    near,
+    paired,
+    far_in,
+    packed,
+    grad_cols,
+    grad_turned,
+    proj_out,
+    proj_in,
+    proj,
+    direction,
+    back_out,
+    back_in,
+    update,
+    returned,
+    load_sem,
+    own_sem,
+    near_sem,
+    far_sem,
+    slot_sem,
+    proj_sem,
+    back_sem,
+    return_sem,
+):
+    replicas, halves, owners, blocks, rows, width, chunks, subs = sizes
+    far = replicas // 2
+    group = halves * owners
+    quarter = width // replicas
+    cols = quarter // chunks
+    sub_rows = rows // subs
+    me_dp = lax.axis_index("dp")
+    me_group = lax.axis_index("half") * owners + lax.axis_index("own")
+    me_far = me_dp // 2
+    parity = me_dp % 2
+    mate = me_far * 2 + 1 - parity
+
+    def dp_id(index):
+        return {"dp": index}
+
+    def group_id(index):
+        return {"half": index // owners, "own": index % owners}
+
+    def remote(src, dst, sems, index_out, index_in, target):
+        return pltpu.make_async_remote_copy(
+            src_ref=src,
+            dst_ref=dst,
+            send_sem=sems.at[(0,) + index_out],
+            recv_sem=sems.at[(1,) + index_in],
+            device_id=target,
+            device_id_type=MESH,
+        )
+
+    def columns(quarter_index, chunk):
+        return pl.ds(pl.multiple_of(quarter_index * quarter + chunk * cols, LANES), cols)
+
+    pieces = [(k, r) for k in range(chunks) for r in range(subs)]
+    order = list(range(1, far)) + [0]
+
+    own_loads = {}
+    for k, r in pieces:
+        for j in order:
+            index = ((me_far + j) % far) * 2 + parity
+            own_loads[j, k, r] = pltpu.make_async_copy(
+                grad.at[:, pl.ds(r * sub_rows, sub_rows), columns(index, k)],
+                own[j][k][r],
+                own_sem.at[j, k, r],
+            )
+            own_loads[j, k, r].start()
+
+    barrier = pltpu.get_barrier_semaphore()
+    for j in range(1, replicas):
+        pl.semaphore_signal(
+            barrier, inc=1, device_id=dp_id((me_dp + j) % replicas), device_id_type=MESH
+        )
+    for t in range(1, group):
+        pl.semaphore_signal(
+            barrier, inc=1, device_id=group_id((me_group + t) % group), device_id_type=MESH
+        )
+    pl.semaphore_wait(barrier, replicas - 1 + group - 1)
+
+    sends = []
+    back_own = {}
+
+    near_copies = {}
+    for k, r in pieces:
+        for j in order:
+            index = ((me_far + j) % far) * 2 + 1 - parity
+            copy = remote(
+                grad.at[:, pl.ds(r * sub_rows, sub_rows), columns(index, k)],
+                near[j][k][r],
+                near_sem,
+                (j, k, r),
+                (j, k, r),
+                dp_id(mate),
+            )
+            copy.start()
+            near_copies[j, k, r] = copy
+            sends.append(copy)
+
+    loads = [
+        pltpu.make_async_copy(left_in.at[0], left, load_sem.at[0]),
+        pltpu.make_async_copy(right_in.at[0], right, load_sem.at[1]),
+        pltpu.make_async_copy(first_in.at[0], first, load_sem.at[2]),
+        pltpu.make_async_copy(second_in.at[0], second, load_sem.at[3]),
+    ]
+    for load in loads:
+        load.start()
+
+    def slot_of(b):
+        owner = table[b, 0]
+        rank = lax.fori_loop(
+            0, b, lambda c, n: n + jnp.where(table[c, 0] == owner, 1, 0), jnp.int32(0)
+        )
+        return rank * owners + owner
+
+    slots = [slot_of(b) for b in range(blocks)]
+    block_of = []
+    for s in range(group):
+        found = jnp.int32(0)
+        for b in range(blocks):
+            found = jnp.where(slots[b] == s, jnp.int32(b), found)
+        block_of.append(found)
+
+    far_copies = {}
+    for k, r in pieces:
+        for j in range(1, far):
+            own_loads[j, k, r].wait()
+            near_copies[j, k, r].wait_recv()
+            for b in range(blocks):
+                paired[j - 1][k][r][b] = (
+                    own[j][k][r][b].astype(jnp.float32) + near[j][k][r][b].astype(jnp.float32)
+                ).astype(jnp.bfloat16)
+            copy = remote(
+                paired[j - 1][k][r],
+                far_in[j - 1][k][r],
+                far_sem,
+                (j - 1, k, r),
+                (j - 1, k, r),
+                dp_id(((me_far + j) % far) * 2 + parity),
+            )
+            copy.start()
+            far_copies[j, k, r] = copy
+            sends.append(copy)
+
+    def pack(k, r):
+        own_loads[0, k, r].wait()
+        near_copies[0, k, r].wait_recv()
+        for j in range(1, far):
+            far_copies[j, k, r].wait_recv()
+        gradients = []
+        for b in range(blocks):
+            total = own[0][k][r][b].astype(jnp.float32) + near[0][k][r][b].astype(jnp.float32)
+            for j in range(1, far):
+                total = total + far_in[j - 1][k][r][b].astype(jnp.float32)
+            gradients.append(total.astype(jnp.bfloat16))
+        for s in range(group):
+            packed[k][r][s] = pick(block_of[s], gradients)
+        here = pl.ds(pl.multiple_of(me_group * rows + r * sub_rows, TILE_ROWS), sub_rows)
+        for t in range(1, group):
+            to = (me_group + t) % group
+            copy = remote(
+                packed[k][r].at[to],
+                grad_cols[k].at[here],
+                slot_sem,
+                (k, r, to),
+                (k, r, me_group),
+                group_id(to),
+            )
+            copy.start()
+            sends.append(copy)
+
+    def project(k):
+        for r in range(subs):
+            for t in range(1, group):
+                source = (me_group + t) % group
+                there = pl.ds(pl.multiple_of(source * rows + r * sub_rows, TILE_ROWS), sub_rows)
+                remote(
+                    packed[k][r].at[source],
+                    grad_cols[k].at[there],
+                    slot_sem,
+                    (k, r, source),
+                    (k, r, source),
+                    group_id(source),
+                ).wait_recv()
+        for r in range(subs):
+            here = pl.ds(pl.multiple_of(me_group * rows + r * sub_rows, TILE_ROWS), sub_rows)
+            grad_cols[k][here] = packed[k][r][me_group]
+        grad_turned[...] = grad_cols[k][...].T
+        for e in range(replicas):
+            proj_out[k][e] = jnp.dot(
+                grad_turned[...],
+                left[:, e * quarter : (e + 1) * quarter],
+                preferred_element_type=jnp.float32,
+            ).astype(jnp.bfloat16)
+        for j in [*range(2, replicas), 1]:
+            to = (me_dp + j) % replicas
+            copy = remote(
+                proj_out[k].at[to],
+                proj_in[k].at[me_dp],
+                proj_sem,
+                (k, to),
+                (k, me_dp),
+                dp_id(to),
+            )
+            copy.start()
+            sends.append(copy)
+
+    def turn(k):
+        for j in range(replicas):
+            source = (me_dp + j) % replicas
+            if j > 0:
+                remote(
+                    proj_out[k].at[source],
+                    proj_in[k].at[source],
+                    proj_sem,
+                    (k, source),
+                    (k, source),
+                    dp_id(source),
+                ).wait_recv()
+        proj_in[k][me_dp] = proj_out[k][me_dp]
+        for e in range(replicas):
+            first_col = e * quarter + k * cols
+            proj[:, first_col : first_col + cols] = proj_in[k][e].T
+
+    for k, r in pieces:
+        pack(k, r)
+    for k in range(chunks):
+        if k == 0:
+            loads[0].wait()
+        project(k)
+    for k in range(chunks):
+        turn(k)
+    for load in loads[1:]:
+        load.wait()
+
+    for e in range(replicas):
+        part = slice(e * quarter, (e + 1) * quarter)
+        rotated = jnp.dot(proj[...], right[:, part], preferred_element_type=jnp.float32)
+        first_new = beta_first * first[:, part].astype(jnp.float32) + (1.0 - beta_first) * rotated
+        second_new = (
+            beta_second * second[:, part].astype(jnp.float32)
+            + (1.0 - beta_second) * rotated * rotated
+        )
+        direction[:, part] = (
+            first_new / bias_first / (jnp.sqrt(second_new / bias_second) + epsilon)
+        ).astype(jnp.bfloat16)
+
+    for k in range(chunks):
+        for j in [*range(2, replicas), 1, 0]:
+            to = (me_dp + j) % replicas
+            these = right[pl.ds(pl.multiple_of(to * quarter + k * cols, LANES), cols), :]
+            result = lax.dot_general(
+                direction[...], these, (((1,), (1,)), ((), ())), preferred_element_type=jnp.float32
+            ).astype(jnp.bfloat16)
+            if j == 0:
+                back_own[k] = result
+            else:
+                back_out[k][j - 1][...] = result
+                copy = remote(
+                    back_out[k][j - 1],
+                    back_in[k].at[me_dp],
+                    back_sem,
+                    (k, to),
+                    (k, me_dp),
+                    dp_id(to),
+                )
+                copy.start()
+                sends.append(copy)
+
+    for k in range(chunks):
+        for j in range(1, replicas):
+            source = (me_dp + j) % replicas
+            remote(
+                back_out[k][j - 1],
+                back_in[k].at[source],
+                back_sem,
+                (k, source),
+                (k, source),
+                dp_id(source),
+            ).wait_recv()
+        back_in[k][me_dp] = back_own[k]
+        update[k][...] = (
+            jnp.dot(
+                left[...], back_in[k][...].reshape(width, cols), preferred_element_type=jnp.float32
+            )
+            .astype(jnp.bfloat16)
+            .reshape(group, rows, cols)
+        )
+        for t in range(1, group):
+            to = (me_group + t) % group
+            copy = remote(
+                update[k].at[to],
+                returned[k].at[me_group],
+                return_sem,
+                (k, to),
+                (k, me_group),
+                group_id(to),
+            )
+            copy.start()
+            sends.append(copy)
+
+    for k in range(chunks):
+        for t in range(1, group):
+            source = (me_group + t) % group
+            remote(
+                update[k].at[source],
+                returned[k].at[source],
+                return_sem,
+                (k, source),
+                (k, source),
+                group_id(source),
+            ).wait_recv()
+        returned[k][me_group] = update[k][me_group]
+        arrived = [returned[k][s] for s in range(group)]
+        for b in range(blocks):
+            out[b, :, k * cols : (k + 1) * cols] = pick(slots[b], arrived)
+
+    for copy in sends:
+        copy.wait_send()
+
+
+def nest(counts, shape):
+    if not counts:
+        return pltpu.VMEM(shape, jnp.bfloat16)
+    return [nest(counts[1:], shape) for _ in range(counts[0])]
+
+
+def fused(grad_parts, owner_table, left_basis, right_basis, first_moment, second_moment):
+    replicas, halves, owners = (lax.axis_size(a) for a in ("dp", "half", "own"))
+    blocks, rows, width = grad_parts.shape[1:]
+    quarter = width // replicas
+    group = halves * owners
+    far = replicas // 2
+    chunks = quarter // LANES
+    subs = 2 if rows % (2 * TILE_ROWS) == 0 else 1
+    cols, sub_rows = quarter // chunks, rows // subs
+    sizes = (replicas, halves, owners, blocks, rows, width, chunks, subs)
+    bf16, dma = jnp.bfloat16, pltpu.SemaphoreType.DMA
+    hbm = pl.BlockSpec(memory_space=pl.ANY)
+    return pl.pallas_call(
+        functools.partial(step_kernel, sizes),
+        out_shape=jax.ShapeDtypeStruct((blocks, rows, quarter), bf16),
+        in_specs=[pl.BlockSpec(memory_space=pltpu.SMEM)] + [hbm] * 5,
+        out_specs=pl.BlockSpec(memory_space=pltpu.VMEM),
+        scratch_shapes=[
+            pltpu.VMEM((width, width), bf16),
+            pltpu.VMEM((width, width), bf16),
+            pltpu.VMEM((quarter, width), bf16),
+            pltpu.VMEM((quarter, width), bf16),
+            nest((far, chunks, subs), (blocks, sub_rows, cols)),
+            nest((far, chunks, subs), (blocks, sub_rows, cols)),
+            nest((far - 1, chunks, subs), (blocks, sub_rows, cols)),
+            nest((far - 1, chunks, subs), (blocks, sub_rows, cols)),
+            nest((chunks, subs), (group, sub_rows, cols)),
+            nest((chunks,), (width, cols)),
+            pltpu.VMEM((cols, width), bf16),
+            nest((chunks,), (replicas, cols, quarter)),
+            nest((chunks,), (replicas, cols, quarter)),
+            pltpu.VMEM((quarter, width), bf16),
+            pltpu.VMEM((quarter, width), bf16),
+            nest((chunks, replicas - 1), (quarter, cols)),
+            nest((chunks,), (replicas, quarter, cols)),
+            nest((chunks,), (group, rows, cols)),
+            nest((chunks,), (group, rows, cols)),
+            dma((4,)),
+            dma((far, chunks, subs)),
+            dma((2, far, chunks, subs)),
+            dma((2, far - 1, chunks, subs)),
+            dma((2, chunks, subs, group)),
+            dma((2, chunks, replicas)),
+            dma((2, chunks, replicas)),
+            dma((2, chunks, group)),
+        ],
+        compiler_params=pltpu.CompilerParams(collective_id=0, has_side_effects=True),
+    )(owner_table, grad_parts.reshape(blocks, rows, width), left_basis, right_basis, first_moment, second_moment)
+
+
+def fits_kernel(mesh, rows, width):
+    replicas = mesh.shape["dp"]
+    return (
+        replicas >= 4
+        and replicas % 2 == 0
+        and rows % TILE_ROWS == 0
+        and width % (replicas * LANES) == 0
+    )
+
+
+def route(mesh, *arrays):
+    rows = arrays[0].shape[2]
+    body = fused if fits_kernel(mesh, rows, arrays[0].shape[3]) else local
+    return body(*arrays)
+
+
 def solution(mesh):
     return jax.shard_map(
-        local,
+        functools.partial(route, mesh),
         mesh=mesh,
         in_specs=(
             P("dp", None, ("half", "own"), None),

time: 162 us -> 57.2 us (0.35)
  waiting for transfers between devices: 75.4 us -> 0 us
  blocking collectives: 57.7 us -> 0 us
  Pallas kernels: 0 us -> 53.9 us
  between operations: 13.2 us -> 0.01 us
  matrix products: 9.55 us -> 0 us
    all_to_all x4 -> x0, blocking collectives: 57.7 us -> none  [the longest x1 18.3 us: local(): lax.all_to_all(lax.all_to_all(outgoing, 'half', split_axis=0, concat_axis...]
    pallas_call x0 -> x1, Pallas kernels: none -> 53.9 us  [fused(): pl.pallas_call(functools.partial(step_kernel, sizes), out_shape=jax.Shape...]
    all_gather x2 -> x0, waiting for transfers between devices: 42.9 us -> none  [the longest x1 22.7 us: local(): lax.all_gather(direction, 'dp', axis=0, tiled=True)]
    reduce_scatter x1 -> x0, waiting for transfers between devices: 31.8 us -> none  [local(): lax.psum_scatter(grad_parts[0].astype(jnp.float32).astype(jnp.bfloat16),...]
    dot_general x4 -> x0, matrix products: 9.55 us -> none  [the longest x1 4.95 us: local(): jnp.dot(projected.astype(jnp.bfloat16), right_matrix, preferred_element_t...]
  transfers between devices with their start and end apart: 3 -> 0, of which waited for: 3 -> 0; matrix products, arithmetic and copies ran while one was open for 1% -> 0% of each run, Pallas kernels for 0% -> 0%
where the time goes in v1:
time: 57.2 us; the launch traced here: 57 us
  Pallas kernels  53.9 us (94%)
  local copies, waits for them, and re-layouts  3.09 us (5%)
    pallas_call x1, Pallas kernels, fused(): pl.pallas_call(functools.partial(step_kernel, sizes), out_shape=jax.Shape...  53.9 us
    unnamed x2, local copies, waits for them, and re-layouts  3.09 us

profile of v1, /device:TPU:0, one launch (start us, length us, event | category | flops | bytes accessed | tf_op | source)
XLA Modules:
  0.0 57.0 jit_solution(3572267162228124942)
XLA Ops:
  0.0 1.3 %copy.7.table = s32[6,1]{1,0:T(8,128)} copy(s32[6,1]{0,1:T(1,128)} %param.7) | data formatting | bytes 48 | tf_op args[1]
  1.3 53.9 %shard_map.64 = bf16[6,128,256]{2,1,0:T(8,128)(2,1)} custom-call(s32[6,1]{1,0:T(8,128)} %copy.7.table, bf16[6,128,1024]{2,1,0:T(8,128)(2,1)} %bitcast.1, bf16[1,1024,1024]{2,1,0:T(8,128)(2,1)} %left_in.1, bf16[1,1024,1024]{2,1,0:T(8,128)(2,1)} %right_in.1, bf16[1,256,1024]{2,1,0:T(8,128)(2,1)} %first_in.1, bf16[1,256,1024]{2,1,0:T(8,128)(2,1)} %second_in.1), custom_call_target="tpu_custom_call" | custom-call | tf_op jit(solution)/shard_map/pallas_call | solution.py:462
  55.3 1.8 %copy.9 = bf16[6,128,256]{2,1,0:T(8,128)(2,1)} copy(bf16[6,128,256]{2,1,0:T(8,128)(2,1)} %shard_map.64) | data formatting | bytes 786432

commit v2 on v1

--- a/solution.py
+++ b/solution.py
@@ -1,4 +1,5 @@
 import functools
+import math
 
 import jax
 import jax.numpy as jnp
@@ -121,6 +122,7 @@
     first,
     second,
     own,
+    lent,
     near,
     paired,
     far_in,
@@ -130,13 +132,16 @@
     proj_out,
     proj_in,
     proj,
+    partial,
     direction,
     back_out,
     back_in,
     update,
     returned,
     load_sem,
+    right_sem,
     own_sem,
+    lent_sem,
     near_sem,
     far_sem,
     slot_sem,
@@ -156,6 +161,17 @@
     parity = me_dp % 2
     mate = me_far * 2 + 1 - parity
 
+    middle = max(1, owners // 2)
+    me_half, me_own = me_group // owners, me_group % owners
+    side = me_own // middle
+    others = []
+    for across in range(owners // middle - 1, -1, -1):
+        for i in range(middle):
+            for h in range(halves):
+                if across or i or h:
+                    o = (side + across) % (owners // middle) * middle + (me_own + i) % middle
+                    others.append((me_half + h) % halves * owners + o)
+
     def dp_id(index):
         return {"dp": index}
 
@@ -178,16 +194,20 @@
     pieces = [(k, r) for k in range(chunks) for r in range(subs)]
     order = list(range(1, far)) + [0]
 
-    own_loads = {}
+    own_loads, lent_loads = {}, {}
     for k, r in pieces:
         for j in order:
-            index = ((me_far + j) % far) * 2 + parity
-            own_loads[j, k, r] = pltpu.make_async_copy(
-                grad.at[:, pl.ds(r * sub_rows, sub_rows), columns(index, k)],
-                own[j][k][r],
-                own_sem.at[j, k, r],
-            )
-            own_loads[j, k, r].start()
+            for side, into, sems, copies in (
+                (1 - parity, lent, lent_sem, lent_loads),
+                (parity, own, own_sem, own_loads),
+            ):
+                index = ((me_far + j) % far) * 2 + side
+                copies[j, k, r] = pltpu.make_async_copy(
+                    grad.at[:, pl.ds(r * sub_rows, sub_rows), columns(index, k)],
+                    into[j][k][r],
+                    sems.at[j, k, r],
+                )
+                copies[j, k, r].start()
 
     barrier = pltpu.get_barrier_semaphore()
     for j in range(1, replicas):
@@ -206,9 +226,9 @@
     near_copies = {}
     for k, r in pieces:
         for j in order:
-            index = ((me_far + j) % far) * 2 + 1 - parity
+            lent_loads[j, k, r].wait()
             copy = remote(
-                grad.at[:, pl.ds(r * sub_rows, sub_rows), columns(index, k)],
+                lent[j][k][r],
                 near[j][k][r],
                 near_sem,
                 (j, k, r),
@@ -221,17 +241,27 @@
 
     loads = [
         pltpu.make_async_copy(left_in.at[0], left, load_sem.at[0]),
-        pltpu.make_async_copy(right_in.at[0], right, load_sem.at[1]),
-        pltpu.make_async_copy(first_in.at[0], first, load_sem.at[2]),
-        pltpu.make_async_copy(second_in.at[0], second, load_sem.at[3]),
+        pltpu.make_async_copy(first_in.at[0], first, load_sem.at[1]),
+        pltpu.make_async_copy(second_in.at[0], second, load_sem.at[2]),
     ]
     for load in loads:
         load.start()
+    right_loads = [
+        pltpu.make_async_copy(
+            right_in.at[0, pl.ds(e * quarter + k * cols, cols)],
+            right[k].at[pl.ds(e * cols, cols)],
+            right_sem.at[k, e],
+        )
+        for k in range(chunks)
+        for e in range(replicas)
+    ]
+    for load in right_loads:
+        load.start()
 
     def slot_of(b):
-        owner = table[b, 0]
+        owner = table[b]
         rank = lax.fori_loop(
-            0, b, lambda c, n: n + jnp.where(table[c, 0] == owner, 1, 0), jnp.int32(0)
+            0, b, lambda c, n: n + jnp.where(table[c] == owner, 1, 0), jnp.int32(0)
         )
         return rank * owners + owner
 
@@ -278,8 +308,7 @@
         for s in range(group):
             packed[k][r][s] = pick(block_of[s], gradients)
         here = pl.ds(pl.multiple_of(me_group * rows + r * sub_rows, TILE_ROWS), sub_rows)
-        for t in range(1, group):
-            to = (me_group + t) % group
+        for to in others:
             copy = remote(
                 packed[k][r].at[to],
                 grad_cols[k].at[here],
@@ -293,8 +322,7 @@
 
     def project(k):
         for r in range(subs):
-            for t in range(1, group):
-                source = (me_group + t) % group
+            for source in others:
                 there = pl.ds(pl.multiple_of(source * rows + r * sub_rows, TILE_ROWS), sub_rows)
                 remote(
                     packed[k][r].at[source],
@@ -341,8 +369,7 @@
                 ).wait_recv()
         proj_in[k][me_dp] = proj_out[k][me_dp]
         for e in range(replicas):
-            first_col = e * quarter + k * cols
-            proj[:, first_col : first_col + cols] = proj_in[k][e].T
+            proj[:, e * cols : (e + 1) * cols] = proj_in[k][e].T
 
     for k, r in pieces:
         pack(k, r)
@@ -350,27 +377,33 @@
         if k == 0:
             loads[0].wait()
         project(k)
+    for load in right_loads + loads[1:]:
+        load.wait()
     for k in range(chunks):
         turn(k)
-    for load in loads[1:]:
-        load.wait()
-
-    for e in range(replicas):
-        part = slice(e * quarter, (e + 1) * quarter)
-        rotated = jnp.dot(proj[...], right[:, part], preferred_element_type=jnp.float32)
-        first_new = beta_first * first[:, part].astype(jnp.float32) + (1.0 - beta_first) * rotated
-        second_new = (
-            beta_second * second[:, part].astype(jnp.float32)
-            + (1.0 - beta_second) * rotated * rotated
-        )
-        direction[:, part] = (
-            first_new / bias_first / (jnp.sqrt(second_new / bias_second) + epsilon)
-        ).astype(jnp.bfloat16)
+        for e in range(replicas):
+            part = slice(e * quarter, (e + 1) * quarter)
+            rotated = jnp.dot(proj[...], right[k][:, part], preferred_element_type=jnp.float32)
+            if k > 0:
+                rotated = rotated + partial[:, part]
+            if k < chunks - 1:
+                partial[:, part] = rotated
+                continue
+            first_new = (
+                beta_first * first[:, part].astype(jnp.float32) + (1.0 - beta_first) * rotated
+            )
+            second_new = (
+                beta_second * second[:, part].astype(jnp.float32)
+                + (1.0 - beta_second) * rotated * rotated
+            )
+            direction[:, part] = (
+                first_new / bias_first / (jnp.sqrt(second_new / bias_second) + epsilon)
+            ).astype(jnp.bfloat16)
 
     for k in range(chunks):
         for j in [*range(2, replicas), 1, 0]:
             to = (me_dp + j) % replicas
-            these = right[pl.ds(pl.multiple_of(to * quarter + k * cols, LANES), cols), :]
+            these = right[k][pl.ds(pl.multiple_of(to * cols, LANES), cols), :]
             result = lax.dot_general(
                 direction[...], these, (((1,), (1,)), ((), ())), preferred_element_type=jnp.float32
             ).astype(jnp.bfloat16)
@@ -408,8 +441,7 @@
             .astype(jnp.bfloat16)
             .reshape(group, rows, cols)
         )
-        for t in range(1, group):
-            to = (me_group + t) % group
+        for to in others:
             copy = remote(
                 update[k].at[to],
                 returned[k].at[me_group],
@@ -422,8 +454,7 @@
             sends.append(copy)
 
     for k in range(chunks):
-        for t in range(1, group):
-            source = (me_group + t) % group
+        for source in others:
             remote(
                 update[k].at[source],
                 returned[k].at[source],
@@ -454,7 +485,7 @@
     group = halves * owners
     far = replicas // 2
     chunks = quarter // LANES
-    subs = 2 if rows % (2 * TILE_ROWS) == 0 else 1
+    subs = math.gcd(rows // TILE_ROWS, 4)
     cols, sub_rows = quarter // chunks, rows // subs
     sizes = (replicas, halves, owners, blocks, rows, width, chunks, subs)
     bf16, dma = jnp.bfloat16, pltpu.SemaphoreType.DMA
@@ -466,9 +497,10 @@
         out_specs=pl.BlockSpec(memory_space=pltpu.VMEM),
         scratch_shapes=[
             pltpu.VMEM((width, width), bf16),
-            pltpu.VMEM((width, width), bf16),
+            nest((chunks,), (replicas * cols, width)),
             pltpu.VMEM((quarter, width), bf16),
             pltpu.VMEM((quarter, width), bf16),
+            nest((far, chunks, subs), (blocks, sub_rows, cols)),
             nest((far, chunks, subs), (blocks, sub_rows, cols)),
             nest((far, chunks, subs), (blocks, sub_rows, cols)),
             nest((far - 1, chunks, subs), (blocks, sub_rows, cols)),
@@ -478,13 +510,16 @@
             pltpu.VMEM((cols, width), bf16),
             nest((chunks,), (replicas, cols, quarter)),
             nest((chunks,), (replicas, cols, quarter)),
-            pltpu.VMEM((quarter, width), bf16),
+            pltpu.VMEM((quarter, replicas * cols), bf16),
+            pltpu.VMEM((quarter, width), jnp.float32),
             pltpu.VMEM((quarter, width), bf16),
             nest((chunks, replicas - 1), (quarter, cols)),
             nest((chunks,), (replicas, quarter, cols)),
             nest((chunks,), (group, rows, cols)),
             nest((chunks,), (group, rows, cols)),
-            dma((4,)),
+            dma((3,)),
+            dma((chunks, replicas)),
+            dma((far, chunks, subs)),
             dma((far, chunks, subs)),
             dma((2, far, chunks, subs)),
             dma((2, far - 1, chunks, subs)),
@@ -494,7 +529,7 @@
             dma((2, chunks, group)),
         ],
         compiler_params=pltpu.CompilerParams(collective_id=0, has_side_effects=True),
-    )(owner_table, grad_parts.reshape(blocks, rows, width), left_basis, right_basis, first_moment, second_moment)
+    )(owner_table.reshape(blocks), grad_parts.reshape(blocks, rows, width), left_basis, right_basis, first_moment, second_moment)
 
 
 def fits_kernel(mesh, rows, width):

time: 57.2 us -> 56 us (0.979)
  local copies, waits for them, and re-layouts: 3.09 us -> 1.77 us
    unnamed x2 -> x1, local copies, waits for them, and re-layouts: 3.09 us -> 1.77 us
where the time goes in v2:
time: 56 us; the launch traced here: 55.8 us
  Pallas kernels  54 us (96%)
  local copies, waits for them, and re-layouts  1.77 us (3%)
    pallas_call x1, Pallas kernels, fused(): pl.pallas_call(functools.partial(step_kernel, sizes), out_shape=jax.Shape...  54 us
    unnamed x1, local copies, waits for them, and re-layouts  1.77 us

profile of v2, /device:TPU:0, one launch (start us, length us, event | category | flops | bytes accessed | tf_op | source)
XLA Modules:
  0.0 55.8 jit_solution(769097432227227784)
XLA Ops:
  0.0 54.0 %shard_map.64 = bf16[6,128,256]{2,1,0:T(8,128)(2,1)} custom-call(s32[6]{0:T(128)} %bitcast.3, bf16[6,128,1024]{2,1,0:T(8,128)(2,1)} %bitcast.2, bf16[1,1024,1024]{2,1,0:T(8,128)(2,1)} %left_in.1, bf16[1,1024,1024]{2,1,0:T(8,128)(2,1)} %right_in.1, bf16[1,256,1024]{2,1,0:T(8,128)(2,1)} %first_in.1, bf16[1,256,1024]{2,1,0:T(8,128)(2,1)} %second_in.1), custom_call_target="tpu_custom_call" | custom-call | tf_op jit(solution)/shard_map/pallas_call | solution.py:493
  54.1 1.8 %copy.8 = bf16[6,128,256]{2,1,0:T(8,128)(2,1)} copy(bf16[6,128,256]{2,1,0:T(8,128)(2,1)} %shard_map.64) | data formatting | bytes 786432
